TPU v7x, 32 devices: a whole 2x2x4 slice. The times are simulated.
32 devices in a mesh: rep: 4 (over y, x), fsdp: 8 (over z, core).
Axes of the slice: x: 2, y: 2, z: 4, core: 2. Of those that a mesh axis runs over, the one named last changes fastest.
Arguments:
- latents: bfloat16 [8, 1024, 1152], P('fsdp', 'rep'), may hold values from -6 to 6
- condition: bfloat16 [8, 1152], P('fsdp'), may hold values from -6 to 6
- adapter_index: int32 [8, 5], P('fsdp'), may hold values from 0 to 7
- weight_mod: bfloat16 [1152, 6912], P('fsdp'), may hold values from -0.1875 to 0.1875
- weight_qkv: bfloat16 [1152, 3456], P('fsdp'), may hold values from -0.1875 to 0.1875
- weight_proj: bfloat16 [1152, 1152], P('fsdp'), may hold values from -3 to 3
- weight_fc1: bfloat16 [1152, 4608], P('fsdp'), may hold values from -0.1875 to 0.1875
- weight_fc2: bfloat16 [4608, 1152], P('fsdp'), may hold values from -0.09375 to 0.09375
- master: float32 [3391488], P('fsdp'), may hold values from -0.25 to 0.25
- moment1: float32 [3391488], P('fsdp'), may hold values from -64 to 64
- moment2: float32 [3391488], P('fsdp'), may hold values from 1 to 1000
- cotangent: bfloat16 [8, 1024, 1152], P('fsdp', 'rep'), may hold values from -6 to 6
Outputs:
- output: bfloat16 [8, 1024, 1152], P('fsdp', 'rep')
- latents_grad: float32 [8, 1024, 1152], P('fsdp', 'rep')
- condition_grad: float32 [8, 1152], P('fsdp')
- new_master: float32 [3391488], P('fsdp')
- new_moment1: float32 [3391488], P('fsdp')
- new_moment2: float32 [3391488], P('fsdp')
- rounded_adapters: bfloat16 [3391488], P('fsdp')
All inputs are finite; a program needn't handle non-finite values.
Results may differ from a plain program's by a relative error of at most 0.03.
The roundings to bfloat16 on the way count: a program that leaves them out, or rounds other values in their place, can miss the bound.
Values may be sent and summed in bfloat16 or wider, within the bound.
A program may use at most 256 MiB of HBM per device.

v0:
```python
import jax
import jax.numpy as jnp
from jax import lax
from jax.sharding import PartitionSpec as P

D = 1152
HEAD_DIM = 72
FF = 4608
RANK = 16
ADAPT = 8
STEP = 3


adapter_scale = 2.0
norm_eps = 1e-06


def adapter_shapes():
    pairs = [(D, 6 * D), (D, 3 * D), (D, D), (D, FF), (FF, D)]
    shapes = []
    for fan_in, fan_out in pairs:
        shapes.append((ADAPT, fan_in, RANK))
        shapes.append((ADAPT, RANK, fan_out))
    return shapes


def unpack(flat):
    tables = []
    offset = 0
    for shape in adapter_shapes():
        count = shape[0] * shape[1] * shape[2]
        tables.append(flat[offset : offset + count].reshape(shape))
        offset = offset + count
    return tables


def norm_modulate(values, shift, scale):
    centred = values - jnp.mean(values, axis=-1, keepdims=True)
    spread = jnp.mean(centred * centred, axis=-1, keepdims=True)
    normed = centred * lax.rsqrt(spread + norm_eps)
    return normed * (1.0 + scale[:, None, :]) + shift[:, None, :]


def gelu_tanh(values):
    return jax.nn.gelu(values, approximate=True)


def shards(
    latents,
    condition,
    adapter_index,
    weight_mod,
    weight_qkv,
    weight_proj,
    weight_fc1,
    weight_fc2,
    master,
    moment1,
    moment2,
    cotangent,
):
    maximal_precision = lax.Precision.HIGHEST
    seqs, tokens, width = latents.shape
    heads = width // HEAD_DIM
    scale = HEAD_DIM ** (-0.5)
    adapters = lax.all_gather(master.astype(jnp.bfloat16), "fsdp", axis=0, tiled=True)
    tables = unpack(adapters)
    select = jax.nn.one_hot(adapter_index, ADAPT, dtype=jnp.float32)
    select_low = select.astype(jnp.bfloat16)
    downs = [
        jnp.einsum(
            "sk,kdr->sdr",
            select_low[:, selected_adapter],
            tables[2 * selected_adapter],
            preferred_element_type=jnp.float32,
        ).astype(jnp.bfloat16)
        for selected_adapter in range(5)
    ]
    raise_factors = [
        jnp.einsum(
            "sk,kro->sro",
            select_low[:, selected_adapter],
            tables[2 * selected_adapter + 1],
            preferred_element_type=jnp.float32,
        ).astype(jnp.bfloat16)
        for selected_adapter in range(5)
    ]

    def adapted(rows_low, weight, selected_adapter):
        inner_lowrank = jnp.einsum(
            "std,sdr->str", rows_low, downs[selected_adapter], preferred_element_type=jnp.float32
        ).astype(jnp.bfloat16)
        additional_term = adapter_scale * jnp.einsum(
            "str,sro->sto",
            inner_lowrank,
            raise_factors[selected_adapter],
            preferred_element_type=jnp.float32,
        )
        return (
            jnp.einsum("std,de->ste", rows_low, weight, preferred_element_type=jnp.float32)
            + additional_term,
            inner_lowrank,
        )

    def adapted_back(grad_low, weight, rows_low, inner_lowrank, selected_adapter):
        raise_gradient = adapter_scale * jnp.einsum(
            "str,sto->sro", inner_lowrank, grad_low, preferred_element_type=jnp.float32
        )
        grad_inner = (
            adapter_scale
            * jnp.einsum(
                "sto,sro->str",
                grad_low,
                raise_factors[selected_adapter],
                preferred_element_type=jnp.float32,
            )
        ).astype(jnp.bfloat16)
        grad_down = jnp.einsum(
            "std,str->sdr", rows_low, grad_inner, preferred_element_type=jnp.float32
        )
        grad_rows = jnp.einsum("ste,de->std", grad_low, weight, preferred_element_type=jnp.float32)
        grad_rows = grad_rows + jnp.einsum(
            "str,sdr->std", grad_inner, downs[selected_adapter], preferred_element_type=jnp.float32
        )
        return (grad_rows, grad_down, raise_gradient)

    cond_full = condition.astype(jnp.float32)
    condition_activated, silu_back = jax.vjp(jax.nn.silu, cond_full)
    silu_low = condition_activated.astype(jnp.bfloat16)
    apply_modulation = jnp.dot(
        silu_low,
        lax.all_gather(weight_mod, "fsdp", axis=0, tiled=True),
        preferred_element_type=jnp.float32,
    )
    inner_modulation = jnp.einsum(
        "sd,sdr->sr", silu_low, downs[0], preferred_element_type=jnp.float32
    ).astype(jnp.bfloat16)
    apply_modulation = apply_modulation + adapter_scale * jnp.einsum(
        "sr,sro->so", inner_modulation, raise_factors[0], preferred_element_type=jnp.float32
    )
    shift_a, scale_a, gate_a, shift_m, scale_m, gate_m = jnp.split(apply_modulation, 6, axis=1)
    attn_weight, proj_weight = (
        lax.all_gather(weight_qkv, "fsdp", axis=0, tiled=True),
        lax.all_gather(weight_proj, "fsdp", axis=0, tiled=True),
    )
    residual_in = latents.astype(jnp.float32)
    first, first_back = jax.vjp(norm_modulate, residual_in, shift_a, scale_a)
    first_low = first.astype(jnp.bfloat16)
    qkv, inner_qkv = adapted(first_low, attn_weight, 1)
    qkv_low = qkv.astype(jnp.bfloat16)
    query = qkv_low[..., :width]
    keys = qkv_low[..., width : 2 * width]
    values = qkv_low[..., 2 * width :]
    keys_all, values_all = (
        lax.all_gather(keys, "rep", axis=1, tiled=True),
        lax.all_gather(values, "rep", axis=1, tiled=True),
    )
    length = keys_all.shape[1]
    latent = 0
    query_heads = query[latent].reshape(tokens, heads, HEAD_DIM)
    key_heads = keys_all[latent].reshape(length, heads, HEAD_DIM)
    value_heads = values_all[latent].reshape(length, heads, HEAD_DIM)
    scores = (
        jnp.einsum("qhe,khe->hqk", query_heads, key_heads, preferred_element_type=jnp.float32)
        * scale
    )
    log_total = jax.nn.logsumexp(scores, axis=-1, keepdims=True)
    probs_low = jnp.exp(scores - log_total).astype(jnp.bfloat16)
    mixed_rows = [
        jnp.einsum(
            "hqk,khe->qhe", probs_low, value_heads, preferred_element_type=jnp.float32
        ).reshape(tokens, width)
    ]
    lse_rows = [log_total]
    mixed_low = jnp.stack(mixed_rows).astype(jnp.bfloat16)
    attn_out, inner_proj = adapted(mixed_low, proj_weight, 2)
    after_attn = residual_in + gate_a[:, None] * attn_out
    expand = lax.all_gather(weight_fc1, "fsdp", axis=0, tiled=True)
    second, second_back = jax.vjp(norm_modulate, after_attn, shift_m, scale_m)
    second_low = second.astype(jnp.bfloat16)
    pre, inner_fc1 = adapted(second_low, expand, 3)
    act, gelu_back = jax.vjp(gelu_tanh, pre)
    act_low = act.astype(jnp.bfloat16)
    contract = lax.all_gather(weight_fc2, "fsdp", axis=0, tiled=True)
    mlp_out, inner_fc2 = adapted(act_low, contract, 4)
    result = after_attn + gate_m[:, None] * mlp_out
    grad_out = cotangent.astype(jnp.float32)
    grad_downs = [None] * 5
    raise_gradient_list = [None] * 5
    d_gate_m = jnp.sum(grad_out * mlp_out, axis=1)
    d_mlp = (grad_out * gate_m[:, None]).astype(jnp.bfloat16)
    d_act, grad_downs[4], raise_gradient_list[4] = adapted_back(
        d_mlp, contract, act_low, inner_fc2, 4
    )
    d_pre = gelu_back(d_act)[0].astype(jnp.bfloat16)
    d_second, grad_downs[3], raise_gradient_list[3] = adapted_back(
        d_pre, expand, second_low, inner_fc1, 3
    )
    d_after, d_shift_m, d_scale_m = second_back(d_second)
    d_after = grad_out + d_after
    d_gate_a = jnp.sum(d_after * attn_out, axis=1)
    d_attn = (d_after * gate_a[:, None]).astype(jnp.bfloat16)
    d_mixed, grad_downs[2], raise_gradient_list[2] = adapted_back(
        d_attn, proj_weight, mixed_low, inner_proj, 2
    )
    d_mixed_low = d_mixed.astype(jnp.bfloat16)
    latent = 0
    query_heads = query[latent].reshape(tokens, heads, HEAD_DIM)
    key_heads = keys_all[latent].reshape(length, heads, HEAD_DIM)
    value_heads = values_all[latent].reshape(length, heads, HEAD_DIM)
    grad_heads = d_mixed_low[latent].reshape(tokens, heads, HEAD_DIM)
    scores = (
        jnp.einsum("qhe,khe->hqk", query_heads, key_heads, preferred_element_type=jnp.float32)
        * scale
    )
    probs = jnp.exp(scores - lse_rows[latent])
    probs_low = probs.astype(jnp.bfloat16)
    d_value_rows = [
        jnp.einsum(
            "hqk,qhe->khe", probs_low, grad_heads, preferred_element_type=jnp.float32
        ).reshape(length, width)
    ]
    d_probs = jnp.einsum(
        "qhe,khe->hqk", grad_heads, value_heads, preferred_element_type=jnp.float32
    )
    centre = jnp.sum(probs * d_probs, axis=-1, keepdims=True)
    d_scores = (probs * (d_probs - centre)).astype(jnp.bfloat16)
    d_query_rows = [
        (
            jnp.einsum("hqk,khe->qhe", d_scores, key_heads, preferred_element_type=jnp.float32)
            * scale
        ).reshape(tokens, width)
    ]
    d_key_rows = [
        (
            jnp.einsum("hqk,qhe->khe", d_scores, query_heads, preferred_element_type=jnp.float32)
            * scale
        ).reshape(length, width)
    ]
    d_keys, d_values = (
        lax.psum_scatter(
            jnp.stack(d_key_rows).astype(jnp.bfloat16), "rep", scatter_dimension=1, tiled=True
        ).astype(jnp.float32),
        lax.psum_scatter(
            jnp.stack(d_value_rows).astype(jnp.bfloat16), "rep", scatter_dimension=1, tiled=True
        ).astype(jnp.float32),
    )
    d_qkv = jnp.concatenate([jnp.stack(d_query_rows), d_keys, d_values], axis=-1).astype(
        jnp.bfloat16
    )
    d_first, grad_downs[1], raise_gradient_list[1] = adapted_back(
        d_qkv, attn_weight, first_low, inner_qkv, 1
    )
    d_input, d_shift_a, d_scale_a = first_back(d_first)
    latents_grad = d_after + d_input
    modulation_partial = jnp.concatenate(
        [d_shift_a, d_scale_a, d_gate_a, d_shift_m, d_scale_m, d_gate_m], axis=1
    )
    raise_modulation = raise_factors[0].astype(jnp.float32)
    down_mod = downs[0].astype(jnp.float32)
    raise_gradient_list[0] = adapter_scale * jnp.einsum(
        "sr,so->sro",
        inner_modulation.astype(jnp.float32),
        modulation_partial,
        precision=maximal_precision,
    )
    inner_portion = adapter_scale * jnp.einsum(
        "gi,gwi->gw", modulation_partial, raise_modulation, precision=maximal_precision
    )
    grad_downs[0] = jnp.einsum(
        "sd,sr->sdr", silu_low.astype(jnp.float32), inner_portion, precision=maximal_precision
    )
    modulation_total = lax.psum(modulation_partial, "rep")
    d_silu = jnp.dot(
        modulation_total,
        lax.all_gather(weight_mod, "fsdp", axis=0, tiled=True).astype(jnp.float32).T,
        precision=maximal_precision,
    )
    inner_combined = adapter_scale * jnp.einsum(
        "gi,gwi->gw", modulation_total, raise_modulation, precision=maximal_precision
    )
    d_silu = d_silu + jnp.einsum(
        "sr,sdr->sd", inner_combined, down_mod, precision=maximal_precision
    )
    condition_grad = silu_back(d_silu)[0]
    pieces = []
    for selected_adapter in range(5):
        pieces.append(
            jnp.einsum(
                "sk,sdr->kdr",
                select[:, selected_adapter],
                grad_downs[selected_adapter],
                precision=maximal_precision,
            ).reshape(-1)
        )
        pieces.append(
            jnp.einsum(
                "sk,sro->kro",
                select[:, selected_adapter],
                raise_gradient_list[selected_adapter],
                precision=maximal_precision,
            ).reshape(-1)
        )
    flat_grad = jnp.concatenate(pieces)
    grad = lax.psum_scatter(
        flat_grad.astype(jnp.bfloat16), "fsdp", scatter_dimension=0, tiled=True
    ).astype(jnp.float32)
    grad = lax.psum(grad, "rep")
    new_moment1 = 0.5 * moment1 + 0.5 * grad
    new_moment2 = 0.5 * moment2 + 0.5 * grad * grad
    first_hat = new_moment1 / (1.0 - 0.5**STEP)
    second_hat = new_moment2 / (1.0 - 0.5**STEP)
    new_master = master - 0.01 * (first_hat / (jnp.sqrt(second_hat) + 1e-08) + 0.1 * master)
    return (
        result.astype(jnp.bfloat16),
        latents_grad,
        condition_grad,
        new_master,
        new_moment1,
        new_moment2,
        new_master.astype(jnp.bfloat16),
    )


def solution(mesh):
    return jax.shard_map(
        shards,
        mesh=mesh,
        in_specs=(
            P("fsdp", "rep", None),
            P("fsdp", None),
            P("fsdp", None),
            P("fsdp", None),
            P("fsdp", None),
            P("fsdp", None),
            P("fsdp", None),
            P("fsdp", None),
            P("fsdp"),
            P("fsdp"),
            P("fsdp"),
            P("fsdp", "rep", None),
        ),
        out_specs=(
            P("fsdp", "rep", None),
            P("fsdp", "rep", None),
            P("fsdp", None),
            P("fsdp"),
            P("fsdp"),
            P("fsdp"),
            P("fsdp"),
        ),
        check_vma=False,
    )
```

profile of v0, /device:TPU:0, one launch (start us, length us, event | category | flops | bytes accessed | tf_op | source)
XLA Modules:
  0.0 1016.1 jit_solution(8816787892493126649)
XLA Ops:
  15.3 66.5 %all-gather.11.cloned.1.call-done = bf16[3391488]{0:T(1024)(128)(2,1)} async-done(((bf16[423936]{0:T(1024)(128)(2,1)}), bf16[3391488]{0:T(1024)(128)(2,1)}) %all-gather.11.cloned.1.call-update) | async-done | bytes 6782992 | tf_op jit(solution)/shard_map/all_gather | solution.py:66
  104.7 121.4 %all-gather.9.cloned.1.call-done = bf16[1152,6912]{1,0:T(8,128)(2,1)} async-done(((bf16[144,6912]{1,0:T(8,128)(2,1)}), bf16[1152,6912]{1,0:T(8,128)(2,1)}) %all-gather.9.cloned.1.call-update) | async-done | bytes 15925264 | tf_op jit(solution)/shard_map/all_gather | solution.py:132
  226.1 7.7 convolution_reduce_fusion
  235.7 68.8 %all-gather.13.cloned.1.call-done = bf16[1152,3456]{1,0:T(8,128)(2,1)} async-done(((bf16[144,3456]{1,0:T(8,128)(2,1)}), bf16[1152,3456]{1,0:T(8,128)(2,1)}) %all-gather.13.cloned.1.call-update) | async-done | bytes 7962640 | tf_op jit(solution)/shard_map/all_gather | solution.py:143
  304.5 5.8 fusion.111
  327.2 8.3 slice.182
  335.4 6.3 multiply_reduce_fusion
  352.1 52.9 %all-gather.23.cloned.1.call-done = bf16[4608,1152]{1,0:T(8,128)(2,1)} async-done(((bf16[576,1152]{1,0:T(8,128)(2,1)}), bf16[4608,1152]{1,0:T(8,128)(2,1)}) %all-gather.23.cloned.1.call-update) | async-done | bytes 10616848 | tf_op jit(solution)/shard_map/all_gather | solution.py:184
  405.0 12.3 %fusion.56 = f32[256,4608]{1,0:T(8,128)} fusion(bf16[4608,1152]{1,0:T(8,128)(2,1)} %all-gather.23.cloned.1.call-done, bf16[1,256,1152]{2,1,0:T(8,128)(2,1)S(1)} %copy-done.13, f32[1152]{0:T(1024)S(1)} %get-tuple-element.13), kind=kOutput, calls=%fused_computation.129 | convolution fusion | flops 2718793728 | bytes 15929856 | tf_op jit(solution)/shard_map/ste,de->std/dot_general | solution.py:121
  417.3 25.6 %all-gather.17.cloned.1.call-done = bf16[1,1024,1152]{2,1,0:T(8,128)(2,1)} async-done(((bf16[1,256,1152]{2,1,0:T(8,128)(2,1)}), bf16[1,1024,1152]{2,1,0:T(8,128)(2,1)}) %all-gather.17.cloned.1.call-update) | async-done | bytes 2359312 | tf_op jit(solution)/shard_map/all_gather | solution.py:155
  442.9 4.3 copy.49
  447.2 35.3 %all-gather.15.cloned.1.call-done = bf16[1,1024,1152]{2,1,0:T(8,128)(2,1)} async-done(((bf16[1,256,1152]{2,1,0:T(8,128)(2,1)}), bf16[1,1024,1152]{2,1,0:T(8,128)(2,1)}) %all-gather.15.cloned.1.call-update) | async-done | bytes 2359312 | tf_op jit(solution)/shard_map/all_gather | solution.py:156
  482.6 4.7 copy.47
  487.3 4.2 multiply_reduce_fusion.2
  502.7 15.6 %all-gather.19.cloned.1.call-done = bf16[1152,1152]{1,0:T(8,128)(2,1)} async-done(((bf16[144,1152]{1,0:T(8,128)(2,1)}), bf16[1152,1152]{1,0:T(8,128)(2,1)}) %all-gather.19.cloned.1.call-update) | async-done | bytes 2654224 | tf_op jit(solution)/shard_map/all_gather | solution.py:144
  523.8 95.7 %all-gather.21.cloned.1.call-done = bf16[1152,4608]{1,0:T(8,128)(2,1)} async-done(((bf16[144,4608]{1,0:T(8,128)(2,1)}), bf16[1152,4608]{1,0:T(8,128)(2,1)}) %all-gather.21.cloned.1.call-update) | async-done | bytes 10616848 | tf_op jit(solution)/shard_map/all_gather | solution.py:178
  619.5 5.9 fusion.113
  627.7 6.4 fusion.11
  649.6 10.5 %convolution_convert_fusion = bf16[16,72,1024]{2,1,0:T(8,128)(2,1)} fusion(bf16[256,16,72]{0,2,1:T(8,128)(2,1)} %bitcast.241, f32[16,256,1024]{2,1,0:T(8,128)} %copy-done, f32[16,256]{1,0:T(8,128)S(1)} %log_add_fusion), kind=kOutput, calls=%fused_computation.50 | convolution fusion | flops 617742336 | bytes 19742720 | tf_op jit(solution)/shard_map/hqk,qhe->khe/dot_general | solution.py:219
  660.1 12.9 %multiply_reduce_fusion.1 = (f32[16,256]{1,0:T(8,128)S(1)}, f32[16,256,1024]{2,1,0:T(8,128)}) fusion(f32[16,256,1024]{2,1,0:T(8,128)} %copy-done, f32[16,256]{1,0:T(8,128)S(1)} %log_add_fusion, bf16[256,16,72]{0,2,1:T(8,128)(2,1)} %bitcast.242, bf16[1024,16,72]{0,2,1:T(8,128)(2,1)} %bitcast.232), kind=kOutput, calls=%fused_computation.3 | convolution fusion | flops 620752896 | bytes 36536320 | tf_op jit(solution)/shard_map/qhe,khe->hqk/dot_general | solution.py:223
  673.1 12.3 %multiply_convert_fusion.1 = bf16[16,256,1024]{2,1,0:T(8,128)(2,1)S(1)} fusion(f32[16,256,1024]{2,1,0:T(8,128)} %get-tuple-element.61, f32[16,256,1024]{2,1,0:T(8,128)} %copy-done, f32[16,256]{1,0:T(8,128)S(1)} %get-tuple-element.60, f32[16,256]{1,0:T(8,128)S(1)} %log_add_fusion), kind=kLoop, calls=%fused_computation.2 | loop fusion | flops 20971520 | bytes 41975808 | tf_op jit(solution)/shard_map/convert_element_type | solution.py:227
  714.5 5.2 multiply_convert_fusion
  719.8 11.3 %reshape.827 = bf16[589824]{0:T(1024)(128)(2,1)} reshape(bf16[8,4608,16]{2,1,0:T(8,128)(2,1)} %multiply_convert_fusion) | data formatting | bytes 2359296 | tf_op jit(solution)/shard_map/reshape | solution.py:294
  731.0 7.0 fusion.24
  738.1 7.2 fusion.114
  749.6 5.9 fusion.101
  759.6 4.0 fusion.33
  794.5 142.3 %all-reduce.6.cloned.1.call-done = bf16[3391488]{0:T(1024)(128)(2,1)} async-done(((bf16[3391488]{0:T(1024)(128)(2,1)}), bf16[3391488]{0:T(1024)(128)(2,1)}) %all-reduce.6.cloned.1.call-update) | async-done | bytes 6782992
  939.3 16.9 %psum.14 = f32[6912]{0:T(1024)S(1)} all-reduce(f32[6912]{0:T(1024)S(1)} %copy-done.55), channel_id=1, replica_groups=mesh['rep'=4,'fsdp'=8] {'rep'}, use_global_device_ids=true, to_apply=%region_19.20 | all-reduce | flops 6912 | bytes 55296 | tf_op jit(solution)/shard_map/psum | solution.py:273
  957.0 15.4 %convolution_reduce_fusion.3 = f32[1152]{0:T(1024)S(1)} fusion(f32[6912,1]{0,1:T(1,128)S(1)} %reshape.860, bf16[1152,6912]{1,0:T(8,128)(2,1)} %all-gather.9.cloned.1.call-done), kind=kOutput, calls=%fused_computation.110 | convolution fusion | flops 95551488 | bytes 15957504 | tf_op jit(solution)/shard_map/dot_general | solution.py:274
  973.1 30.4 %all-reduce.4.cloned.1.call-done = f32[423936]{0:T(1024)} async-done(((f32[423936]{0:T(1024)}), f32[423936]{0:T(1024)}) %all-reduce.4.cloned.1.call-update) | async-done | bytes 1695760 | tf_op jit(solution)/shard_map/psum | solution.py:308
  1003.6 5.5 fusion.103
  (397 shorter events, 164.9 us)
Async XLA Ops:
  7.2 74.5 %all-gather.11.cloned.1.call-start = ((), (), s32[]{:S(2)}) async-start(), calls=%async_computation.3 | async-start | bytes 7630848 | tf_op jit(solution)/shard_map/all_gather | solution.py:66
  9.7 216.4 %all-gather.9.cloned.1.call-start = ((), (), s32[]{:S(2)}) async-start(), calls=%async_computation.2 | async-start | bytes 17915904 | tf_op jit(solution)/shard_map/all_gather | solution.py:132
  10.5 294.0 %all-gather.13.cloned.1.call-start = ((), (), s32[]{:S(2)}) async-start(), calls=%async_computation.4 | async-start | bytes 8957952 | tf_op jit(solution)/shard_map/all_gather | solution.py:143
  11.2 393.8 %all-gather.23.cloned.1.call-start = ((), (), s32[]{:S(2)}) async-start(), calls=%async_computation.9 | async-start | bytes 11943936 | tf_op jit(solution)/shard_map/all_gather | solution.py:184
  11.8 431.2 %all-gather.17.cloned.1.call-start = ((), (), s32[]{:S(2)}) async-start(), calls=%async_computation.6 | async-start | bytes 2949120 | tf_op jit(solution)/shard_map/all_gather | solution.py:155
  12.0 222.5 %copy-start.78 = (f32[256]{0:T(256)}, f32[256]{0:T(256)S(1)}, u32[]{:S(2)}) copy-start(f32[256]{0:T(256)S(1)} %broadcast_multiply_fusion.2) | copy-start | bytes 3076
  12.3 72.4 %copy-start.94 = (f32[256]{0:T(256)}, f32[256]{0:T(256)S(1)}, u32[]{:S(2)}) copy-start(f32[256]{0:T(256)S(1)} %fusion.30) | copy-start | bytes 3076
  104.0 206.2 %copy-start.45 = (bf16[1,16,3456]{2,0,1:T(2,128)(2,1)}, bf16[1,16,3456]{2,0,1:T(2,128)(2,1)S(1)}, u32[]{:S(2)}) copy-start(bf16[1,16,3456]{2,0,1:T(2,128)(2,1)S(1)} %fusion.48) | copy-start | bytes 331780
  104.7 130.7 %copy-start.24 = (bf16[1152,16]{1,0:T(8,128)(2,1)}, bf16[1152,16]{1,0:T(8,128)(2,1)S(1)}, u32[]{:S(2)}) copy-start(bf16[1152,16]{1,0:T(8,128)(2,1)S(1)} %multiply_reduce_fusion.5) | copy-start | bytes 110596
  104.7 130.4 %copy-start.86 = (f32[256]{0:T(256)S(1)}, f32[256]{0:T(256)}, u32[]{:S(2)}) copy-start(f32[256]{0:T(256)} %fusion.81) | copy-start | bytes 3076
  234.5 170.5 %copy-start.69 = (f32[1152]{0:T(1024)}, f32[1152]{0:T(1024)S(1)}, u32[]{:S(2)}) copy-start(f32[1152]{0:T(1024)S(1)} %get-tuple-element.13) | copy-start | bytes 13828
  235.4 74.8 %copy-start.16 = (bf16[256,1152]{1,0:T(8,128)(2,1)}, bf16[256,1152]{1,0:T(8,128)(2,1)S(1)}, u32[]{:S(2)}) copy-start(bf16[256,1152]{1,0:T(8,128)(2,1)S(1)} %fusion.53) | copy-start | bytes 1769476
  235.7 74.6 %copy-start.80 = (bf16[256,16]{0,1:T(8,128)(2,1)}, bf16[256,16]{0,1:T(8,128)(2,1)S(1)}, u32[]{:S(2)}) copy-start(bf16[256,16]{0,1:T(8,128)(2,1)S(1)} %convolution_convert_fusion.4) | copy-start | bytes 24580
  312.3 170.3 %all-gather.15.cloned.1.call-start = ((), (), s32[]{:S(2)}) async-start(), calls=%async_computation.5 | async-start | bytes 2949120 | tf_op jit(solution)/shard_map/all_gather | solution.py:156
  312.8 205.4 %all-gather.19.cloned.1.call-start = ((), (), s32[]{:S(2)}) async-start(), calls=%async_computation.7 | async-start | bytes 2985984 | tf_op jit(solution)/shard_map/all_gather | solution.py:144
  313.6 305.9 %all-gather.21.cloned.1.call-start = ((), (), s32[]{:S(2)}) async-start(), calls=%async_computation.8 | async-start | bytes 11943936 | tf_op jit(solution)/shard_map/all_gather | solution.py:178
  314.3 431.0 %reduce-scatter.5.cloned.1.call-start = ((), (), s32[]{:S(2)}) async-start(), calls=%async_computation.11 | async-start | bytes 2949120 | tf_op jit(solution)/shard_map/reduce_scatter | solution.py:244
  347.7 154.1 %copy-start.26 = (bf16[1152,16]{1,0:T(8,128)(2,1)}, bf16[1152,16]{1,0:T(8,128)(2,1)S(1)}, u32[]{:S(2)}) copy-start(bf16[1152,16]{1,0:T(8,128)(2,1)S(1)} %multiply_reduce_fusion.4) | copy-start | bytes 110596
  501.8 19.3 %copy-start.11 = (bf16[16,72,256]{2,1,0:T(8,128)(2,1)}, bf16[16,72,256]{2,1,0:T(8,128)(2,1)S(1)}, u32[]{:S(2)}) copy-start(bf16[16,72,256]{2,1,0:T(8,128)(2,1)S(1)} %convolution_convert_fusion.1) | copy-start | bytes 1769476
  523.5 101.9 %copy-start.18 = (bf16[256,1152]{1,0:T(8,128)(2,1)}, bf16[256,1152]{1,0:T(8,128)(2,1)S(1)}, u32[]{:S(2)}) copy-start(bf16[256,1152]{1,0:T(8,128)(2,1)S(1)} %fusion.50) | copy-start | bytes 1769476
  523.8 101.7 %copy-start.43 = (bf16[1,16,4608]{2,0,1:T(2,128)(2,1)S(1)}, bf16[1,16,4608]{2,0,1:T(2,128)(2,1)}, u32[]{:S(2)}) copy-start(bf16[1,16,4608]{2,0,1:T(2,128)(2,1)} %fusion.38) | copy-start | bytes 442372
  627.6 15.4 %copy-start.4 = (bf16[256,4608]{1,0:T(8,128)(2,1)}, bf16[256,4608]{1,0:T(8,128)(2,1)S(1)}, u32[]{:S(2)}) copy-start(bf16[256,4608]{1,0:T(8,128)(2,1)S(1)} %get-tuple-element.57) | copy-start | bytes 7077892
  660.1 85.2 %reduce-scatter.3.cloned.1.call-start = ((), (), s32[]{:S(2)}) async-start(), calls=%async_computation.10 | async-start | bytes 2949120 | tf_op jit(solution)/shard_map/reduce_scatter | solution.py:241
  690.7 246.1 %all-reduce.6.cloned.1.call-start = ((), (), s32[]{:S(2)}) async-start(), calls=%async_computation.13 | async-start | bytes 13565952
  792.6 146.7 %copy-start.55 = (f32[6912]{0:T(1024)S(1)}, f32[6912]{0:T(1024)}, u32[]{:S(2)}) copy-start(f32[6912]{0:T(1024)} %copy-done.54) | copy-start | bytes 82948
  792.6 163.6 %copy-start.49 = (bf16[1,16,6912]{2,0,1:T(2,128)(2,1)S(1)}, bf16[1,16,6912]{2,0,1:T(2,128)(2,1)}, u32[]{:S(2)}) copy-start(bf16[1,16,6912]{2,0,1:T(2,128)(2,1)} %copy-done.47) | copy-start | bytes 663556
  792.6 163.9 %copy-start.39 = (bf16[1152,16]{1,0:T(8,128)(2,1)S(1)}, bf16[1152,16]{1,0:T(8,128)(2,1)}, u32[]{:S(2)}) copy-start(bf16[1152,16]{1,0:T(8,128)(2,1)} %copy-done.38) | copy-start | bytes 110596
  792.7 210.9 %all-reduce.4.cloned.1.call-start = ((), (), s32[]{:S(2)}) async-start(), calls=%async_computation.12 | async-start | bytes 3391488 | tf_op jit(solution)/shard_map/psum | solution.py:308
  957.0 15.5 %copy-start.74 = (bf16[1,1152]{1,0:T(2,128)(2,1)S(1)}, bf16[1,1152]{1,0:T(2,128)(2,1)}, u32[]{:S(2)}) copy-start(bf16[1,1152]{1,0:T(2,128)(2,1)} %param.13) | copy-start | bytes 6916
  957.0 15.5 %copy-start.76 = (f32[1,1152]{1,0:T(1,128)S(1)}, f32[1,1152]{1,0:T(1,128)}, u32[]{:S(2)}) copy-start(f32[1,1152]{1,0:T(1,128)} %get-tuple-element.24) | copy-start | bytes 13828
  957.0 46.5 %copy-start.10 = (f32[423936]{0:T(1024)S(1)}, f32[423936]{0:T(1024)}, u32[]{:S(2)}) copy-start(f32[423936]{0:T(1024)} %param.20) | copy-start | bytes 5087236
  957.0 46.5 %copy-start.30 = (f32[423936]{0:T(1024)S(1)}, f32[423936]{0:T(1024)}, u32[]{:S(2)}) copy-start(f32[423936]{0:T(1024)} %param.21) | copy-start | bytes 5087236
  (102 other events, 369.4 us)
Sparse Core Ops, SparseCore 0:
  10.2 71.4 all-gather.10
  83.3 142.6 all-gather.8
  227.7 76.6 all-gather.12
  306.0 98.9 all-gather.22
  407.2 35.6 all-gather.16
  445.2 37.3 all-gather.14
  484.2 33.9 all-gather.18
  519.9 99.5 all-gather.20
  660.2 35.6 reduce-scatter.4
  698.8 37.3 reduce-scatter.2
  792.7 144.0 all-reduce.5
  940.4 63.0 all-reduce.3
where the time goes:
time: 1030 us; the launch traced here: 1020 us
  waiting for transfers between devices  658 us (64%)
  matrix products  148 us (14%)
  local copies, waits for them, and re-layouts  109 us (11%)
  other arithmetic  66.9 us (6%)
  blocking collectives  16.9 us (2%)
  between operations  16.7 us (2%)
    unnamed x13, waiting for transfers between devices  146 us
    all_gather x1, waiting for transfers between devices, shards(): lax.all_gather(weight_mod, 'fsdp', axis=0, tiled=True)  121 us
    all_gather x1, waiting for transfers between devices, shards(): expand = lax.all_gather(weight_fc1, 'fsdp', axis=0, tiled=True)  95.7 us
    all_gather x1, waiting for transfers between devices, shards(): lax.all_gather(weight_qkv, 'fsdp', axis=0, tiled=True)  68.8 us
    all_gather x1, waiting for transfers between devices, shards(): lax.all_gather(master.astype(jnp.bfloat16), 'fsdp', axis=0, tiled=True)  66.5 us
    all_gather x1, waiting for transfers between devices, shards(): contract = lax.all_gather(weight_fc2, 'fsdp', axis=0, tiled=True)  52.9 us
    all_gather x1, waiting for transfers between devices, shards(): lax.all_gather(values, 'rep', axis=1, tiled=True)  35.3 us
    slice x13, local copies, waits for them, and re-layouts, unpack(): tables.append(flat[offset:offset + count].reshape(shape))  31.5 us
  transfers between devices with their start and end apart: 12, of which 10 were waited for; matrix products, arithmetic and copies ran while one was open for 22% of the time, Pallas kernels for 0%

commit v1 on v0

v1 whole, which is shorter than its diff:
```python
import functools

import jax
import jax.numpy as jnp
from jax import lax
from jax.experimental import pallas as pl
from jax.experimental.pallas import tpu as pltpu
from jax.sharding import PartitionSpec as P

D = 1152
HEAD_DIM = 72
HEADS = 16
FF = 4608
RANK = 16
ADAPT = 8
STEP = 3
NORM_EPS = 1e-06
F32 = jnp.float32
BF16 = jnp.bfloat16
PAIRS = ((D, 6 * D), (D, 3 * D), (D, D), (D, FF), (FF, D))


def dot(a, b, dims, **kw):
    return lax.dot_general(a, b, (dims, ((), ())), preferred_element_type=F32, **kw)


def mm(a, b):
    return dot(a, b, ((1,), (0,)))


def mm_t(a, b):
    return dot(a, b, ((1,), (1,)))


def tmm(a, b):
    return dot(a, b, ((0,), (0,)))


def low(v):
    return v.astype(BF16)


def layer_norm(v):
    centred = v - jnp.mean(v, axis=-1, keepdims=True)
    inv = lax.rsqrt(jnp.mean(centred * centred, axis=-1, keepdims=True) + NORM_EPS)
    return centred * inv, inv


def layer_norm_back(g, normed, inv):
    m1 = jnp.mean(g, axis=-1, keepdims=True)
    m2 = jnp.mean(g * normed, axis=-1, keepdims=True)
    return inv * (g - m1 - normed * m2)


LANE = 128
GELU_C = 0.7978845608028654
GELU_A = 0.044715


def tile_sum(v):
    shift = LANE // 2
    while shift >= RANK:
        v = v + pltpu.roll(v, shift, 1)
        shift //= 2
    return v


def rep_copy(src, dst, send, recv, peer):
    return pltpu.make_async_remote_copy(src_ref=src, dst_ref=dst, send_sem=send, recv_sem=recv,
                                        device_id={"rep": peer}, device_id_type=pl.DeviceIdType.MESH)


def rep_barrier(R, r):
    sem = pltpu.get_barrier_semaphore()
    for i in range(1, R):
        pl.semaphore_signal(sem, inc=1, device_id={"rep": lax.rem(r + i, R)}, device_id_type=pl.DeviceIdType.MESH)
    pl.semaphore_wait(sem, R - 1)


def block(i, n):
    return pl.ds(pl.multiple_of(i * n, n), n)


def attn_fwd_kernel(R, hl, scale, lat_ref, dout_ref, mods_ref, wqkv_ref, z1_ref, bt1_ref, wproj_ref, z2_ref, bt2_ref,
                    h1_ref, u1_ref, qkv_ref, lse_ref, mixed_ref, u2_ref, ao_ref, x1_ref, h2a_ref, douta_ref,
                    wq, vt, osc, msend, mrecv, ds_sem, dr_sem, ms_sem, mr_sem, hs_sem, hr_sem):
    r = lax.axis_index("rep")
    T = dout_ref.shape[0]
    L = T * R
    cw = hl * HEAD_DIM
    rep_barrier(R, r)
    douta_ref[block(r, T), :] = dout_ref[...]

    def dcopy(i, who):
        return rep_copy(dout_ref, douta_ref.at[block(who, T)], ds_sem.at[i], dr_sem.at[who], lax.rem(r + i, R))

    for i in range(1, R):
        dcopy(i, r).start()
    wq[...] = jnp.zeros_like(wq)
    for i in range(3 * hl):
        wq[:, i * LANE:i * LANE + HEAD_DIM] = wqkv_ref[:, i * HEAD_DIM:(i + 1) * HEAD_DIM]
    shift_a, scale_a, gate_a = mods_ref[0:1, :], mods_ref[1:2, :], mods_ref[2:3, :]
    shift_m, scale_m = mods_ref[3:4, :], mods_ref[4:5, :]

    def first(c, _):
        rows = block(c, T)
        n, _ = layer_norm(lat_ref[rows, :].astype(F32))
        h1 = low(n * (1.0 + scale_a) + shift_a)
        h1_ref[rows, :] = h1
        u1 = low(tile_sum(mm(h1, z1_ref[...])))
        u1_ref[rows, :] = u1
        u1 = u1 * BF16(0.25)
        for j in range(3):
            cols = pl.ds(j * hl * LANE, hl * LANE)
            qkv_ref[rows, cols] = low(mm(h1, wq[:, cols]) + mm(u1, bt1_ref[:, cols]))
        return 0

    lax.fori_loop(0, R, first, 0)

    def transpose_v(h, _):
        vt[block(h, LANE), :] = qkv_ref[:, block(2 * hl + h, LANE)].T
        return 0

    lax.fori_loop(0, hl, transpose_v, 0)

    def mcopy(i, who):
        peer = lax.rem(r + i, R)
        return rep_copy(msend.at[block(peer, T)], mrecv.at[who], ms_sem.at[i], mr_sem.at[who], peer)

    def attend(i, _):
        peer = lax.rem(r + 1 + i, R)
        rows = block(peer, T)

        def head(h, _):
            s = mm_t(qkv_ref[:, block(hl + h, LANE)], qkv_ref[rows, block(h, LANE)])
            top = jnp.max(s, axis=0, keepdims=True)
            e = jnp.exp((s - top) * scale)
            total = jnp.sum(e, axis=0, keepdims=True)
            lse_ref[block(h, 8), rows] = jnp.broadcast_to(top * scale + jnp.log(total), (8, T))
            o = mm(vt[block(h, LANE), :], low(e * (1.0 / total)))
            osc[h] = o.T
            return 0

        lax.fori_loop(0, hl, head, 0)
        for h in range(hl):
            msend[rows, h * HEAD_DIM:(h + 1) * HEAD_DIM] = low(osc[h][:, :HEAD_DIM])

        @pl.when(i < R - 1)
        def _():
            mcopy(i + 1, r).start()
        return 0

    lax.fori_loop(0, R, attend, 0)
    mrecv[r] = msend[block(r, T), :]
    for i in range(1, R):
        mcopy(i, lax.rem(r + i, R)).wait_recv()
    for p in range(R):
        mixed_ref[:, p * cw:(p + 1) * cw] = mrecv[p]
    mixed = mixed_ref[...]
    u2 = low(tile_sum(mm(mixed, z2_ref[...])))
    u2_ref[...] = u2
    ao = mm(mixed, wproj_ref[...]) + mm(u2 * BF16(0.25), bt2_ref[...])
    ao_ref[...] = ao
    x1 = lat_ref[block(r, T), :].astype(F32) + gate_a * ao
    x1_ref[...] = x1
    n, _ = layer_norm(x1)
    h2a_ref[block(r, T), :] = low(n * (1.0 + scale_m) + shift_m)

    def hcopy(i, who):
        return rep_copy(h2a_ref.at[block(r, T)], h2a_ref.at[block(who, T)], hs_sem.at[i], hr_sem.at[who], lax.rem(r + i, R))

    for i in range(1, R):
        hcopy(i, r).start()
    for i in range(1, R):
        p = lax.rem(r + i, R)
        hcopy(i, p).wait_recv()
        dcopy(i, p).wait_recv()
        dcopy(i, r).wait_send()
        mcopy(i, r).wait_send()
        hcopy(i, r).wait_send()


def mlp_kernel(R, h2a_ref, douta_ref, mods_ref, w1_ref, z3_ref, bt3_ref, w2_ref, z4_ref, bt4_ref, x1_ref,
               out_ref, dx1_ref, dmod_ref, da3_ref, db3_ref, da4_ref, db4_ref,
               act, gp, u3s, u4s, du4s, du3s, dpre, psend, precv, pown, gsend, grecv, gown,
               ps_sem, pr_sem, gs_sem, gr_sem):
    r = lax.axis_index("rep")
    T = x1_ref.shape[0]
    rep_barrier(R, r)
    scale_m, gate_m = mods_ref[4:5, :], mods_ref[5:6, :]

    def pcopy(i, who):
        peer = lax.rem(r + i, R)
        return rep_copy(psend.at[block(peer, T)], precv.at[who], ps_sem.at[i], pr_sem.at[who], peer)

    def gcopy(i, who):
        peer = lax.rem(r + i, R)
        return rep_copy(gsend.at[block(peer, T)], grecv.at[who], gs_sem.at[i], gr_sem.at[who], peer)

    def forward(i, _):
        peer = lax.rem(r + 1 + i, R)
        rows = block(peer, T)
        h2 = h2a_ref[rows, :]
        u3 = low(tile_sum(mm(h2, z3_ref[...])))
        u3s[rows, :] = u3
        x = mm(h2, w1_ref[...]) + mm(u3 * BF16(0.25), bt3_ref[...])
        x2 = x * x
        t = jnp.tanh(GELU_C * (x + GELU_A * x * x2))
        a = low(0.5 * x * (1.0 + t))
        act[rows, :] = a
        gp[rows, :] = 0.5 * (1.0 + t) + 0.5 * x * (1.0 - t * t) * (GELU_C * (1.0 + 3.0 * GELU_A * x2))
        u4 = low(tile_sum(mm(a, z4_ref[...])))
        u4s[rows, :] = u4
        part = mm(a, w2_ref[...]) + mm(u4 * BF16(0.25), bt4_ref[...])
        psend[rows, :] = low(part)
        pown[...] = part

        @pl.when(i < R - 1)
        def _():
            pcopy(i + 1, r).start()
        return 0

    lax.fori_loop(0, R, forward, 0)

    def backward(i, _):
        peer = lax.rem(r + 1 + i, R)
        rows = block(peer, T)
        dm = low(douta_ref[rows, :].astype(F32) * gate_m)
        douta_ref[rows, :] = dm
        du4 = low(2.0 * mm_t(dm, bt4_ref[...]))
        du4s[rows, :] = du4
        d_act = mm_t(dm, w2_ref[...]) + mm_t(du4, z4_ref[...])
        dp = low(d_act * gp[rows, :])
        dpre[rows, :] = dp
        du3 = low(2.0 * mm_t(dp, bt3_ref[...]))
        du3s[rows, :] = du3
        part = mm_t(dp, w1_ref[...]) + mm_t(du3, z3_ref[...])
        gsend[rows, :] = low(part)
        gown[...] = part

        @pl.when(i < R - 1)
        def _():
            gcopy(i + 1, r).start()
        return 0

    dout = douta_ref[block(r, T), :].astype(F32)
    lax.fori_loop(0, R, backward, 0)
    da4_ref[...] = tmm(du4s[...], act[...])[:RANK]
    db4_ref[...] = 2.0 * tmm(u4s[...], douta_ref[...])[:RANK]
    da3_ref[...] = tmm(du3s[...], h2a_ref[...])[:RANK]
    db3_ref[...] = 2.0 * tmm(u3s[...], dpre[...])[:RANK]
    mlp = pown[...]
    for i in range(1, R):
        p = lax.rem(r + i, R)
        pcopy(i, p).wait_recv()
        mlp = mlp + precv[p].astype(F32)
    x1 = x1_ref[...]
    out_ref[...] = low(x1 + gate_m * mlp)
    dmod_ref[...] = jnp.zeros_like(dmod_ref)
    dmod_ref[2:3, :] = jnp.sum(dout * mlp, axis=0, keepdims=True)
    n2, inv2 = layer_norm(x1)
    dh2 = gown[...]
    for i in range(1, R):
        p = lax.rem(r + i, R)
        gcopy(i, p).wait_recv()
        dh2 = dh2 + grecv[p].astype(F32)
    dmod_ref[0:1, :] = jnp.sum(dh2, axis=0, keepdims=True)
    dmod_ref[1:2, :] = jnp.sum(dh2 * n2, axis=0, keepdims=True)
    dx1_ref[...] = dout + layer_norm_back(dh2 * (1.0 + scale_m), n2, inv2)
    for i in range(1, R):
        pcopy(i, r).wait_send()
        gcopy(i, r).wait_send()


def attn_bwd_kernel(R, hl, scale, dx1_ref, ao_ref, mods_ref, wproj_ref, z2_ref, bt2_ref, mixed_ref, u2_ref,
                    qkv_ref, lse_ref, wqkv_ref, z1_ref, bt1_ref, h1_ref, u1_ref, lat_ref,
                    lg_ref, dmod_ref, da2_ref, db2_ref, da1_ref, db1_ref,
                    wq, kt, msend, mrecv, mpad, dkv, dqkv, du1s, gsend, grecv, gown,
                    ms_sem, mr_sem, gs_sem, gr_sem):
    r = lax.axis_index("rep")
    T = dx1_ref.shape[0]
    cw = hl * HEAD_DIM
    rep_barrier(R, r)
    scale_a, gate_a = mods_ref[1:2, :], mods_ref[2:3, :]
    dx1 = dx1_ref[...]
    dmod_ref[...] = jnp.zeros_like(dmod_ref)
    dmod_ref[2:3, :] = jnp.sum(dx1 * ao_ref[...], axis=0, keepdims=True)
    da = low(dx1 * gate_a)
    du2 = low(2.0 * mm_t(da, bt2_ref[...]))
    dm = low(mm_t(da, wproj_ref[...]) + mm_t(du2, z2_ref[...]))
    for p in range(R):
        msend[p] = dm[:, p * cw:(p + 1) * cw]

    def mcopy(i, who):
        peer = lax.rem(r + i, R)
        return rep_copy(msend.at[peer], mrecv.at[who], ms_sem.at[i], mr_sem.at[who], peer)

    for i in range(1, R):
        mcopy(i, r).start()
    mrecv[r] = msend[r]
    db2_ref[...] = 2.0 * tmm(u2_ref[...], da)[:RANK]
    da2_ref[...] = tmm(du2, mixed_ref[...])[:RANK]
    wq[...] = jnp.zeros_like(wq)
    for i in range(3 * hl):
        wq[:, i * LANE:i * LANE + HEAD_DIM] = wqkv_ref[:, i * HEAD_DIM:(i + 1) * HEAD_DIM]

    def transpose_k(h, _):
        kt[block(h, LANE), :] = qkv_ref[:, block(hl + h, LANE)].T
        return 0

    lax.fori_loop(0, hl, transpose_k, 0)
    dkv[...] = jnp.zeros_like(dkv)
    mpad[...] = jnp.zeros_like(mpad)

    def attend(i, _):
        p = lax.rem(r + i, R)

        @pl.when(i > 0)
        def _():
            mcopy(i, p).wait_recv()
        for h in range(hl):
            mpad[h, :, :HEAD_DIM] = mrecv[p][:, h * HEAD_DIM:(h + 1) * HEAD_DIM]
        rows = block(p, T)

        def head(h, _):
            q = qkv_ref[rows, block(h, LANE)]
            g = mpad[h]
            s = mm_t(qkv_ref[:, block(hl + h, LANE)], q)
            lse = lse_ref[block(h, 8), rows][0:1, :]
            probs = jnp.exp(s * scale - lse)
            dkv[:, block(hl + h, LANE)] += mm(low(probs), g)
            dp = mm_t(qkv_ref[:, block(2 * hl + h, LANE)], g)
            centre = jnp.sum(probs * dp, axis=0, keepdims=True)
            ds = low(probs * (dp - centre))
            dkv[:, block(h, LANE)] += mm(ds, q)
            dq = mm(kt[block(h, LANE), :], ds)
            dqkv[rows, block(h, LANE)] = low(dq.T * scale)
            return 0

        lax.fori_loop(0, hl, head, 0)
        return 0

    lax.fori_loop(0, R, attend, 0)

    def gcopy(i, who):
        peer = lax.rem(r + i, R)
        return rep_copy(gsend.at[block(peer, T)], grecv.at[who], gs_sem.at[i], gr_sem.at[who], peer)

    def backward(i, _):
        peer = lax.rem(r + 1 + i, R)
        rows = block(peer, T)
        dqkv[rows, hl * LANE:2 * hl * LANE] = low(dkv[rows, :hl * LANE] * scale)
        dqkv[rows, 2 * hl * LANE:] = low(dkv[rows, hl * LANE:])
        g = dqkv[rows, :]
        du1 = low(2.0 * mm_t(g, bt1_ref[...]))
        du1s[rows, :] = du1
        part = mm_t(g, wq[...]) + mm_t(du1, z1_ref[...])
        gsend[rows, :] = low(part)
        gown[...] = part

        @pl.when(i < R - 1)
        def _():
            gcopy(i + 1, r).start()
        return 0

    lax.fori_loop(0, R, backward, 0)
    da1_ref[...] = tmm(du1s[...], h1_ref[...])[:RANK]
    db1_ref[...] = 2.0 * tmm(u1_ref[...], dqkv[...])[:RANK]
    n1, inv1 = layer_norm(lat_ref[...].astype(F32))
    dh1 = gown[...]
    for i in range(1, R):
        p = lax.rem(r + i, R)
        gcopy(i, p).wait_recv()
        dh1 = dh1 + grecv[p].astype(F32)
    dmod_ref[0:1, :] = jnp.sum(dh1, axis=0, keepdims=True)
    dmod_ref[1:2, :] = jnp.sum(dh1 * n1, axis=0, keepdims=True)
    lg_ref[...] = dx1_ref[...] + layer_norm_back(dh1 * (1.0 + scale_a), n1, inv1)
    for i in range(1, R):
        mcopy(i, r).wait_send()
        gcopy(i, r).wait_send()


def sds(shape, dtype):
    return jax.ShapeDtypeStruct(shape, dtype)


def dma(n):
    return pltpu.SemaphoreType.DMA((n,))


def call(body, cid, out_shape, scratch, *args):
    vm = pl.BlockSpec(memory_space=pltpu.VMEM)
    return pl.pallas_call(body, out_shape=out_shape, in_specs=[vm] * len(args), out_specs=[vm] * len(out_shape),
                          scratch_shapes=scratch,
                          compiler_params=pltpu.CompilerParams(collective_id=cid, has_side_effects=True,
                                                               vmem_limit_bytes=63 * 2 ** 20))(*args)


def spread_down(a):
    n = a.shape[0]
    keep = (jnp.arange(n) % 8)[:, None] == (jnp.arange(LANE) // RANK)[None, :]
    return jnp.where(keep, jnp.tile(a, (1, 8)), jnp.zeros((), a.dtype))


def shards(latents, condition, adapter_index, weight_mod, weight_qkv, weight_proj, weight_fc1, weight_fc2,
           master, moment1, moment2, cotangent):
    R = lax.axis_size("rep")
    F = lax.axis_size("fsdp")
    r = lax.axis_index("rep")
    f = lax.axis_index("fsdp")
    T = latents.shape[1]
    L = T * R
    hl = HEADS // R
    cw = hl * HEAD_DIM
    fw = FF // (F * R)
    rows = weight_qkv.shape[0]
    scale = HEAD_DIM ** -0.5

    def gather(x, axis_name, axis=0):
        return lax.all_gather(x, axis_name, axis=axis, tiled=True)

    def pick(x, axis):
        return lax.dynamic_index_in_dim(x, r, axis, keepdims=False)

    wqkv = gather(pick(weight_qkv.reshape(rows, 3, R, cw), 2).reshape(rows, 3 * cw), "fsdp")
    wproj = gather(weight_proj, "fsdp")
    w1 = gather(pick(weight_fc1.reshape(rows, F, R, fw), 2).reshape(rows, F * fw), "fsdp")
    w2 = gather(pick(weight_fc2.reshape(R, fw, D), 0), "fsdp")
    flat = gather(master.astype(BF16), "fsdp")
    A, B = [], []
    off = 0
    for j, (a, b) in enumerate(PAIRS):
        n = a * RANK
        A.append(lax.dynamic_slice(flat, (off + adapter_index[0, j] * n,), (n,)).reshape(a, RANK))
        off += ADAPT * n
        n = b * RANK
        B.append(lax.dynamic_slice(flat, (off + adapter_index[0, j] * n,), (n,)).reshape(RANK, b))
        off += ADAPT * n
    B1 = jnp.pad(pick(B[1].reshape(RANK, 3, R, hl, HEAD_DIM), 2), ((0, 0), (0, 0), (0, 0), (0, LANE - HEAD_DIM)))
    B1 = B1.reshape(RANK, 3 * hl * LANE)
    B3 = pick(B[3].reshape(RANK, F, R, fw), 2).reshape(RANK, F * fw)
    A4 = pick(A[4].reshape(F, R, fw, RANK), 1).reshape(F * fw, RANK)
    bt1, bt2, bt3, bt4 = [jnp.tile(x, (8, 1)) for x in (B1, B[2], B3, B[4])]
    z1, z2, z3, z4 = [spread_down(x) for x in (A[1], A[2], A[3], A4)]

    cond = condition.astype(F32)
    sig = jax.nn.sigmoid(cond)
    cs = low(cond * sig)
    cs_all = gather(cs, "fsdp")
    cs_mine = lax.dynamic_slice(cs_all, (0, f * rows), (F, rows))
    mod = lax.psum_scatter(mm(cs_mine, weight_mod), "fsdp", scatter_dimension=0, tiled=True)
    u0 = low(mm(cs, A[0]))
    mod = mod + 2.0 * mm(u0, B[0])
    mods = jnp.pad(mod.reshape(6, D), ((0, 2), (0, 0)))

    lat_all = gather(latents[0], "rep")
    FW = F * fw
    W3 = 3 * hl * LANE
    h1, u1, qkv, lse, mixed, u2, ao, x1, h2a, douta = call(
        functools.partial(attn_fwd_kernel, R, hl, scale), 1,
        [sds((L, D), BF16), sds((L, LANE), BF16), sds((L, W3), BF16), sds((hl * 8, L), F32), sds((T, D), BF16),
         sds((T, LANE), BF16), sds((T, D), F32), sds((T, D), F32), sds((L, D), BF16), sds((L, D), BF16)],
        [pltpu.VMEM((D, W3), BF16), pltpu.VMEM((hl * LANE, L), BF16), pltpu.VMEM((hl, T, LANE), F32),
         pltpu.VMEM((L, cw), BF16), pltpu.VMEM((R, T, cw), BF16)] + [dma(R)] * 6,
        lat_all, cotangent[0], mods, wqkv, z1, bt1, wproj, z2, bt2)
    out, dx1, dmod_m, dA3, dB3, dA4, dB4 = call(
        functools.partial(mlp_kernel, R), 2,
        [sds((T, D), BF16), sds((T, D), F32), sds((8, D), F32), sds((RANK, D), F32), sds((RANK, FW), F32),
         sds((RANK, FW), F32), sds((RANK, D), F32)],
        [pltpu.VMEM((L, FW), BF16), pltpu.VMEM((L, FW), F32)] + [pltpu.VMEM((L, LANE), BF16)] * 4
        + [pltpu.VMEM((L, FW), BF16)]
        + [pltpu.VMEM((L, D), BF16), pltpu.VMEM((R, T, D), BF16), pltpu.VMEM((T, D), F32)] * 2 + [dma(R)] * 4,
        h2a, douta, mods, w1, z3, bt3, w2, z4, bt4, x1)
    lg, dmod_a, dA2, dB2, dA1, dB1 = call(
        functools.partial(attn_bwd_kernel, R, hl, scale), 3,
        [sds((T, D), F32), sds((8, D), F32), sds((RANK, D), F32), sds((RANK, D), F32), sds((RANK, D), F32),
         sds((RANK, W3), F32)],
        [pltpu.VMEM((D, W3), BF16), pltpu.VMEM((hl * LANE, L), BF16), pltpu.VMEM((R, T, cw), BF16),
         pltpu.VMEM((R, T, cw), BF16), pltpu.VMEM((hl, T, LANE), BF16), pltpu.VMEM((L, 2 * hl * LANE), F32),
         pltpu.VMEM((L, W3), BF16), pltpu.VMEM((L, LANE), BF16), pltpu.VMEM((L, D), BF16), pltpu.VMEM((R, T, D), BF16),
         pltpu.VMEM((T, D), F32)] + [dma(R)] * 4,
        dx1, ao, mods, wproj, z2, bt2, mixed, u2, qkv, lse, wqkv, z1, bt1, h1, u1, latents[0])
    hi = dict(precision=lax.Precision.HIGHEST)
    d_mod = jnp.concatenate([dmod_a[0:3], dmod_m[0:3]], axis=0).reshape(1, 6 * D)
    d_mod = lax.psum(d_mod, "rep")
    du0 = 2.0 * dot(d_mod, B[0].astype(F32), ((1,), (1,)), **hi)
    dB0 = 2.0 * tmm(u0.astype(F32), d_mod)
    dA0 = tmm(cs.astype(F32), du0)
    d_mod_all = gather(d_mod, "fsdp")
    d_cs = dot(d_mod_all, weight_mod.astype(F32), ((1,), (1,)), **hi)
    d_cs = lax.all_to_all(d_cs, "fsdp", split_axis=0, concat_axis=1, tiled=True)
    d_cs = d_cs + dot(du0, A[0].astype(F32), ((1,), (1,)), **hi)
    condition_grad = d_cs * (sig * (1.0 + cond * (1.0 - sig)))
    one = (r == 0).astype(F32)

    def spread(x, shape, axis):
        full = jnp.zeros(shape, F32)
        return lax.dynamic_update_slice_in_dim(full, jnp.expand_dims(x, axis), r, axis)

    dB1 = dB1.reshape(RANK, 3, hl, LANE)[..., :HEAD_DIM].reshape(RANK, 3, cw)
    dB1f = spread(dB1, (RANK, 3, R, cw), 2)
    dB3f = spread(dB3.reshape(RANK, F, fw), (RANK, F, R, fw), 2)
    dA4f = spread(dA4.T.reshape(F, fw, RANK), (F, R, fw, RANK), 1)
    full = [dA0 * one, dB0 * one, dA1.T, dB1f, dA2.T, dB2, dA3.T, dB3f, dA4f, dB4]
    pieces = []
    for i, g in enumerate(full):
        sel = jax.nn.one_hot(adapter_index[0, i // 2], ADAPT, dtype=F32)
        pieces.append((sel[:, None] * g.reshape(1, -1)).reshape(-1))
    grad = lax.psum_scatter(jnp.concatenate(pieces).astype(BF16), "fsdp", scatter_dimension=0, tiled=True).astype(F32)
    grad = lax.psum(grad, "rep")
    nm1 = 0.5 * moment1 + 0.5 * grad
    nm2 = 0.5 * moment2 + 0.5 * grad * grad
    c = 1.0 - 0.5 ** STEP
    nm = master - 0.01 * ((nm1 / c) / (jnp.sqrt(nm2 / c) + 1e-08) + 0.1 * master)
    return (out[None], lg[None], condition_grad, nm, nm1, nm2, nm.astype(BF16))


def solution(mesh):
    tok = P("fsdp", "rep", None)
    row = P("fsdp", None)
    vec = P("fsdp")
    return jax.shard_map(shards, mesh=mesh,
                         in_specs=(tok, row, row, row, row, row, row, row, vec, vec, vec, tok),
                         out_specs=(tok, tok, row, vec, vec, vec, vec), check_vma=False)
```

time: 1030 us -> 733 us (0.71)
  waiting for transfers between devices: 658 us -> 363 us
  Pallas kernels: 0 us -> 206 us
  matrix products: 148 us -> 3.74 us
  local copies, waits for them, and re-layouts: 109 us -> 58 us
  other arithmetic: 66.9 us -> 21.6 us
  blocking collectives: 16.9 us -> 47.3 us
    all_gather x8 -> x6, waiting for transfers between devices: 482 us -> 128 us  [gather(): return lax.all_gather(x, axis_name, axis=axis, tiled=True)]
    pallas_call x0 -> x3, Pallas kernels: none -> 206 us  [call(): pl.pallas_call(body, out_shape=out_shape, in_specs=[vm] * len(args), out_...]
    dot_general x50 -> x6, matrix products: 148 us -> 3.74 us  [dot(): lax.dot_general(a, b, (dims, ((), ())), preferred_element_type=F32, **kw)]
    unnamed x13 -> x11, waiting for transfers between devices: 146 us -> 192 us
    reshape x12 -> x8, local copies, waits for them, and re-layouts: 42.8 us -> 8.64 us  [the longest x1 5 us: shards(): weight_fc1.reshape(rows, F, R, fw)]
    slice x15 -> x3, local copies, waits for them, and re-layouts: 34 us -> 1.44 us  [the longest x1 0.77 us: shards(): dmod_a[0:3]]
    all_gather x0 -> x2, blocking collectives: none -> 30.2 us  [gather(): return lax.all_gather(x, axis_name, axis=axis, tiled=True)]
    another operation x12 -> x1, other arithmetic: 17.5 us -> 0.01 us
  transfers between devices with their start and end apart: 12 -> 10, of which waited for: 10 -> 8; matrix products, arithmetic and copies ran while one was open for 22% -> 5% of each run, Pallas kernels for 0% -> 10%
where the time goes in v1:
time: 733 us; the launch traced here: 725 us
  waiting for transfers between devices  363 us (50%)
  Pallas kernels  206 us (28%)
  local copies, waits for them, and re-layouts  58 us (8%)
  blocking collectives  47.3 us (6%)
  other arithmetic  21.6 us (3%)
  between operations  21.6 us (3%)
    pallas_call x3, Pallas kernels, call(): pl.pallas_call(body, out_shape=out_shape, in_specs=[vm] * len(args), out_...  206 us
    unnamed x11, waiting for transfers between devices  192 us
    all_gather x6, waiting for transfers between devices, gather(): return lax.all_gather(x, axis_name, axis=axis, tiled=True)  128 us
    psum x1, waiting for transfers between devices, shards(): grad = lax.psum(grad, 'rep')  37.5 us
    all_gather x2, blocking collectives, gather(): return lax.all_gather(x, axis_name, axis=axis, tiled=True)  30.2 us
    unnamed x87, local copies, waits for them, and re-layouts  20.4 us
    psum x1, blocking collectives, shards(): d_mod = lax.psum(d_mod, 'rep')  17.1 us
  transfers between devices with their start and end apart: 10, of which 8 were waited for; matrix products, arithmetic and copies ran while one was open for 5% of the time, Pallas kernels for 10%

profile of v1, /device:TPU:0, one launch (start us, length us, event | category | flops | bytes accessed | tf_op | source)
XLA Modules:
  0.0 725.2 jit_solution(7791085422455951704)
XLA Ops:
  7.2 2.6 convert_element_type.75
  10.0 15.9 %all-gather.2 = bf16[8,1,1152]{2,1,0:T(2,128)(2,1)S(1)} all-gather(bf16[1,1,1152]{2,1,0:T(2,128)(2,1)S(1)} %convert_bitcast_fusion), channel_id=1, replica_groups=mesh['rep'=4,'fsdp'=8] {'fsdp'}, dimensions={0}, use_global_device_ids=true | all-gather | bytes 20736 | tf_op jit(solution)/shard_map/all_gather | solution.py:420
  28.0 2.3 dynamic-slice_reduce_fusion.1
  32.5 5.0 reshape.244
  37.6 3.8 dynamic-slice_reduce_fusion
  41.3 1.2 reshape.245
  42.6 1.7 constant_dynamic-slice_fusion.1
  55.8 25.9 %all-gather.11.cloned.1.call-done = bf16[3391488]{0:T(1024)(128)(2,1)} async-done(((bf16[423936]{0:T(1024)(128)(2,1)}), bf16[3391488]{0:T(1024)(128)(2,1)}) %all-gather.11.cloned.1.call-update) | async-done | bytes 6782992 | tf_op jit(solution)/shard_map/all_gather | solution.py:420
  87.6 48.5 %all-reduce.10.cloned.1.call-done = f32[8,6912]{1,0:T(8,128)} async-done(((f32[8,6912]{1,0:T(8,128)}), f32[8,6912]{1,0:T(8,128)}) %all-reduce.10.cloned.1.call-update) | async-done | bytes 221200
  136.1 1.7 fusion.16
  140.0 1.2 compare_select_fusion
  141.2 27.7 %all-gather.13.cloned.1.call-done.wqkv_ref = bf16[1152,864]{1,0:T(8,128)(2,1)} async-done(((bf16[144,864]{1,0:T(8,128)(2,1)}), bf16[1152,864]{1,0:T(8,128)(2,1)}) %all-gather.13.cloned.1.call-update) | async-done | bytes 1990672 | tf_op jit(solution)/shard_map/all_gather | solution.py:420
  168.9 38.5 %all-gather.19.cloned.1.call-done = bf16[1,1024,1152]{2,1,0:T(8,128)(2,1)} async-done(((bf16[1,256,1152]{2,1,0:T(8,128)(2,1)}), bf16[1,1024,1152]{2,1,0:T(8,128)(2,1)}) %all-gather.19.cloned.1.call-update) | async-done | bytes 2359312 | tf_op jit(solution)/shard_map/all_gather | solution.py:420
  207.4 35.5 %all-gather.15.cloned.1.call-done.wproj_ref = bf16[1152,1152]{1,0:T(8,128)(2,1)} async-done(((bf16[144,1152]{1,0:T(8,128)(2,1)}), bf16[1152,1152]{1,0:T(8,128)(2,1)}) %all-gather.15.cloned.1.call-update) | async-done | bytes 2654224 | tf_op jit(solution)/shard_map/all_gather | solution.py:420
  244.4 76.0 %shard_map.171 = (bf16[1024,1152]{1,0:T(8,128)(2,1)}, bf16[1024,128]{1,0:T(8,128)(2,1)}, bf16[1024,1536]{1,0:T(8,128)(2,1)}, f32[32,1024]{1,0:T(8,128)}, bf16[25...) custom-call(bf16[1024,1152]{1,0:T(8,128)(2,1)} %bitcast.116, ...), custom_call_target="tpu_custom_call" | custom-call | tf_op jit(solution)/shard_map/pallas_call | solution.py:393
  322.0 64.2 %shard_map.172 = (bf16[256,1152]{1,0:T(8,128)(2,1)}, f32[256,1152]{1,0:T(8,128)}, f32[8,1152]{1,0:T(8,128)}, f32[16,1152]{1,0:T(8,128)}, f32[16,1152]{1,0:T(8,12...) custom-call(bf16[1024,1152]{1,0:T(8,128)(2,1)} %get-tuple-element.30.h2a_ref, ...), custom_call_target="tpu_custom_call" | custom-call | tf_op jit(solution)/shard_map/pallas_call | solution.py:393
  386.2 65.6 %shard_map.173 = (f32[256,1152]{1,0:T(8,128)}, f32[8,1152]{1,0:T(8,128)}, f32[16,1152]{1,0:T(8,128)}, f32[16,1152]{1,0:T(8,128)}, f32[16,1152]{1,0:T(8,128)}, /*index=5*/f32[16,1536]{1,0:T(8,128)}) custom-call(f32[256,1152]{1,0:T(8,128)} %get-tuple-element.34.dx1_ref, f32[256,1152]{1,0:T(8,128)} %get-tuple-element.35.ao_ref, f32[8,1152]{1,0:T(8,128)} %pad.8.mods_ref, ...), custom_call_target="tpu_custom_call" | custom-call | tf_op jit(solution)/shard_map/pallas_call | solution.py:393
  452.6 17.1 %psum.14 = f32[1,6912]{1,0:T(1,128)S(1)} all-reduce(f32[1,6912]{1,0:T(1,128)S(1)} %bitcast.135), channel_id=1, replica_groups=mesh['rep'=4,'fsdp'=8] {'rep'}, use_global_device_ids=true, to_apply=%region_1.2 | all-reduce | flops 6912 | bytes 55296 | tf_op jit(solution)/shard_map/psum | solution.py:485
  471.9 1.5 copy.84
  481.2 1.8 dynamic_update_slice.10
  486.7 1.3 mul.349
  488.0 1.2 fusion.3
  489.2 1.2 copy.91
  491.1 1.4 constant_dynamic-update-slice_fusion.8
  500.2 142.5 %all-reduce.12.cloned.1.call-done = bf16[3391488]{0:T(1024)(128)(2,1)} async-done(((bf16[3391488]{0:T(1024)(128)(2,1)}), bf16[3391488]{0:T(1024)(128)(2,1)}) %all-reduce.12.cloned.1.call-update) | async-done | bytes 6782992
  642.7 2.4 dynamic-slice_convert_fusion
  645.2 14.3 %all-gather.3 = f32[8,1,6912]{2,1,0:T(1,128)S(1)} all-gather(f32[1,1,6912]{2,1,0:T(1,128)S(1)} %bitcast.134), channel_id=1, replica_groups=mesh['rep'=4,'fsdp'=8] {'fsdp'}, dimensions={0}, use_global_device_ids=true | all-gather | bytes 248832 | tf_op jit(solution)/shard_map/all_gather | solution.py:420
  659.4 1.6 convolution_bitcast_fusion
  661.7 3.6 all-to-all-start
  665.8 5.2 all-to-all-done
  671.7 37.5 %all-reduce.8.cloned.1.call-done = f32[423936]{0:T(1024)} async-done(((f32[423936]{0:T(1024)}), f32[423936]{0:T(1024)}) %all-reduce.8.cloned.1.call-update) | async-done | bytes 1695760 | tf_op jit(solution)/shard_map/psum | solution.py:510
  709.2 6.5 fusion.25
  (205 shorter events, 47.1 us)
Async XLA Ops:
  7.2 2.7 copy-start.25
  7.2 18.8 %copy-start = (bf16[144,6912]{1,0:T(8,128)(2,1)S(1)}, bf16[144,6912]{1,0:T(8,128)(2,1)}, u32[]{:S(2)}) copy-start(bf16[144,6912]{1,0:T(8,128)(2,1)} %param.15) | copy-start | bytes 5971972
  7.2 74.5 %all-gather.11.cloned.1.call-start = ((), (), s32[]{:S(2)}) async-start(), calls=%async_computation.1 | async-start | bytes 7630848 | tf_op jit(solution)/shard_map/all_gather | solution.py:420
  9.8 17.3 %copy-start.13 = (bf16[144,3456]{1,0:T(8,128)(2,1)S(1)}, bf16[144,3456]{1,0:T(8,128)(2,1)}, u32[]{:S(2)}) copy-start(bf16[144,3456]{1,0:T(8,128)(2,1)} %param.16) | copy-start | bytes 2985988
  9.8 126.3 %all-reduce.10.cloned.1.call-start = ((), (), s32[]{:S(2)}) async-start(), calls=%async_computation.8 | async-start | bytes 442368
  27.1 141.8 %all-gather.13.cloned.1.call-start = ((), (), s32[]{:S(2)}) async-start(), calls=%async_computation.2 | async-start | bytes 2322432 | tf_op jit(solution)/shard_map/all_gather | solution.py:420
  31.3 176.1 %all-gather.19.cloned.1.call-start = ((), (), s32[]{:S(2)}) async-start(), calls=%async_computation.6 | async-start | bytes 2949120 | tf_op jit(solution)/shard_map/all_gather | solution.py:420
  31.9 211.0 %all-gather.15.cloned.1.call-start = ((), (), s32[]{:S(2)}) async-start(), calls=%async_computation.3 | async-start | bytes 2985984 | tf_op jit(solution)/shard_map/all_gather | solution.py:420
  32.5 288.0 %all-gather.17.cloned.1.call-start = ((), (), s32[]{:S(2)}) async-start(), calls=%async_computation.4 | async-start | bytes 2985984 | tf_op jit(solution)/shard_map/all_gather | solution.py:420
  37.5 7.4 %copy-start.26 = (s32[1,5]{1,0:T(1,128)S(1)}, s32[1,5]{1,0:T(1,128)}, u32[]{:S(2)}) copy-start(s32[1,5]{1,0:T(1,128)} %param.14) | copy-start | bytes 64
  37.5 13.9 %copy-start.31 = (u32[32]{0:T(128)S(1)}, u32[32]{0:T(128)}, u32[]{:S(2)}) copy-start(u32[32]{0:T(128)} %constant.170) | copy-start | bytes 388
  42.6 277.9 %all-gather.21.cloned.1.call-start = ((), (), s32[]{:S(2)}) async-start(), calls=%async_computation.7 | async-start | bytes 2985984 | tf_op jit(solution)/shard_map/all_gather | solution.py:420
  44.4 598.3 %all-reduce.12.cloned.1.call-start = ((), (), s32[]{:S(2)}) async-start(), calls=%async_computation.9 | async-start | bytes 13565952
  86.3 52.2 %dynamic-slice-start.1 = ((bf16[3391488]{0:T(1024)(128)(2,1)}, s32[]{:T(128)}), bf16[55296]{0:T(1024)(128)(2,1)S(1)}, s32[]{:S(2)}) async-start(bf16[3391488]{0:T(1024)(128)(2,1)} %all-gather.11.cloned.1.call-done, s32[]{:T(128)} %select_n.112), calls=%async_computation.11 | async-start | bytes 221696 | tf_op jit(solution)/shard_map/dynamic_slice | solution.py:437
  87.0 54.2 %copy-start.7 = (bf16[1152,16]{1,0:T(8,128)(2,1)}, bf16[1152,16]{1,0:T(8,128)(2,1)S(1)}, u32[]{:S(2)}) copy-start(bf16[1152,16]{1,0:T(8,128)(2,1)S(1)} %reshape.239) | copy-start | bytes 110596
  386.2 66.4 %copy-start.27 = (f32[8,1152]{1,0:T(8,128)S(1)}, f32[8,1152]{1,0:T(8,128)}, u32[]{:S(2)}) copy-start(f32[8,1152]{1,0:T(8,128)} %get-tuple-element.44) | copy-start | bytes 110596
  474.8 2.6 copy-start.23
  477.4 2.2 copy-start.22
  477.8 3.0 copy-start.18
  488.0 2.4 copy-start.19
  488.0 2.4 copy-start.28
  491.1 2.1 copy-start.4
  492.5 2.5 copy-start.11
  492.5 3.2 copy-start.12
  494.2 3.3 copy-start.3
  499.4 209.8 %all-reduce.8.cloned.1.call-start = ((), (), s32[]{:S(2)}) async-start(), calls=%async_computation.5 | async-start | bytes 3391488 | tf_op jit(solution)/shard_map/psum | solution.py:510
  500.1 145.0 %copy-start.16 = (f32[1,6912]{1,0:T(1,128)S(1)}, f32[1,6912]{1,0:T(1,128)}, u32[]{:S(2)}) copy-start(f32[1,6912]{1,0:T(1,128)} %copy-done.15) | copy-start | bytes 82948
  500.2 159.3 %copy-start.1 = (bf16[144,6912]{1,0:T(8,128)(2,1)S(1)}, bf16[144,6912]{1,0:T(8,128)(2,1)}, u32[]{:S(2)}) copy-start(bf16[144,6912]{1,0:T(8,128)(2,1)} %param.15) | copy-start | bytes 5971972
  645.1 20.2 %copy-start.8 = (bf16[1152,16]{1,0:T(8,128)(2,1)S(1)}, bf16[1152,16]{1,0:T(8,128)(2,1)}, u32[]{:S(2)}) copy-start(bf16[1152,16]{1,0:T(8,128)(2,1)} %copy-done.7) | copy-start | bytes 110596
  645.1 20.2 %copy-start.30 = (f32[16]{0:T(128)S(1)}, f32[16]{0:T(128)}, u32[]{:S(2)}) copy-start(f32[16]{0:T(128)} %copy-done.29) | copy-start | bytes 196
  661.7 9.2 %all-to-all-start = ((f32[8,1,144]{2,1,0:T(1,128)}), f32[8,1,144]{2,1,0:T(1,128)S(1)}, u32[]{:S(2)}, u32[]{:S(2)}) async-start(f32[8,1,144]{2,1,0:T(1,128)} %copy.65), calls=%async_computation | async-start | bytes 16384 | tf_op jit(solution)/shard_map/all_to_all | solution.py:491
  671.7 44.0 %copy-start.14 = (bf16[256,1152]{1,0:T(8,128)(2,1)S(1)}, bf16[256,1152]{1,0:T(8,128)(2,1)}, u32[]{:S(2)}) copy-start(bf16[256,1152]{1,0:T(8,128)(2,1)} %get-tuple-element.33) | copy-start | bytes 1769476
  (12 other events, 18.3 us)
Sparse Core Ops, SparseCore 0:
  10.2 71.4 all-gather.10
  84.6 51.4 all-reduce.9
  138.3 30.5 all-gather.12
  170.6 36.7 all-gather.18
  208.9 33.9 all-gather.14
  245.0 33.0 all-gather.16
  280.3 33.0 all-gather.20
  499.6 143.0 all-reduce.11
  646.4 62.7 all-reduce.7
